TPU v7x, 128 devices: a whole 4x4x4 slice. The times are simulated.
128 devices in a mesh: col: 16 (over z, y), row: 8 (over x, core).
Axes of the slice: x: 4, y: 4, z: 4, core: 2. Of those that a mesh axis runs over, the one named last changes fastest.
Arguments:
- t_amp: float32 [1024, 20736], P('row', 'col')
- d_denom: float32 [1024, 20736], P('row', 'col')
- v_oovv: bfloat16 [1024, 20736], P('row', 'col')
- v_vvvv: bfloat16 [20736, 20736], P('row', 'col')
- v_oooo: bfloat16 [1024, 1024], replicated
- w_ovov: bfloat16 [4608, 4608], P(None, 'col')
Outputs:
- output: float32 [4608, 4608], P('row', 'col')
All inputs are finite; a program needn't handle non-finite values.
Results may differ from a plain program's by a relative error of at most 0.001.
Values are sent between devices in bfloat16 or wider.
A program may use at most 1 GiB of HBM per device.

v0:
```python
import math
import jax
import jax.numpy as jnp
from jax import lax
from jax.sharding import PartitionSpec as P


def solution(mesh):
    row_n = mesh.shape["row"]
    col_n = mesh.shape["col"]

    def local_sweep(t_blk, d_blk, voovv_blk, vvvvv_blk, oooo_blk, wr_blk):
        n_occ = math.isqrt(oooo_blk.shape[0])
        n_vir = wr_blk.shape[0] // n_occ
        occ_r = n_occ // row_n
        occ_c = n_occ // col_n
        vir_c = n_vir // col_n
        t_bf = t_blk.astype(jnp.bfloat16)
        t_rows = lax.all_gather(t_bf, "col", axis=1, tiled=True)
        t_ladder = lax.all_to_all(t_rows, "row", 1, 0, tiled=True)
        ladder_part = jnp.dot(t_ladder, vvvvv_blk, preferred_element_type=jnp.float32)
        r_ladder = lax.psum_scatter(ladder_part, "row", scatter_dimension=0, tiled=True)
        t_cols = lax.all_gather(t_bf, "row", axis=0, tiled=True)
        x_part = lax.dot_general(voovv_blk, t_cols, (((1,), (1,)), ((), ())), preferred_element_type=jnp.float32)
        x_rows = lax.psum(x_part, "col")
        x_cols = lax.all_to_all(x_rows, "row", 1, 0, tiled=True)
        w_hole = (oooo_blk.astype(jnp.float32) + 0.5 * x_cols).astype(jnp.bfloat16)
        r_hole = lax.dot_general(w_hole, t_cols, (((0,), (0,)), ((), ())), preferred_element_type=jnp.float32)
        amp_four = t_rows.reshape(occ_r, n_occ, n_vir, n_vir)
        wr_three = wr_blk.reshape(n_occ, n_vir, occ_c * n_vir)
        r_mixed = jnp.einsum("ikac,kcn->ian", amp_four, wr_three, preferred_element_type=jnp.float32)
        r_mixed = r_mixed.reshape(occ_r, n_vir, occ_c, n_vir)
        mixed_entry = lax.all_to_all(r_mixed, "col", 1, 2, tiled=True)
        swap_rows = lax.all_to_all(mixed_entry, "row", 2, 0, tiled=True)
        swap_full = lax.all_to_all(swap_rows, "col", 3, 1, tiled=True)
        mixed_image = jnp.transpose(swap_full, (2, 3, 0, 1))
        base_sum = (voovv_blk.astype(jnp.float32) + r_ladder + r_hole).reshape(occ_r, n_occ, vir_c, n_vir)
        d_four = d_blk.reshape(occ_r, n_occ, vir_c, n_vir)
        total_sum = (jnp.transpose(base_sum, (0, 2, 1, 3)) + mixed_entry + mixed_image) / jnp.transpose(d_four, (0, 2, 1, 3))
        t_pairs = lax.all_to_all(total_sum, "col", 2, 1, tiled=True)
        return t_pairs.reshape(occ_r * n_vir, occ_c * n_vir)

    return jax.shard_map(
        local_sweep,
        mesh=mesh,
        in_specs=(P("row", "col"), P("row", "col"), P("row", "col"), P("row", "col"), P(None, "row"), P(None, "col")),
        out_specs=P("row", "col"),
        check_vma=False,
    )
```

profile of v0, /device:TPU:1, one launch (start us, length us, event | category | flops | bytes accessed | tf_op | source)
XLA Modules:
  0.0 347.1 jit_solution(1523196705925051971)
XLA Ops:
  9.2 59.6 %all-gather.3.cloned.1.call-done = bf16[128,20736]{0,1:T(8,128)(2,1)} async-done(((bf16[128,1296]{0,1:T(8,128)(2,1)}), bf16[128,20736]{0,1:T(8,128)(2,1)}) %all-gather.3.cloned.1.call-update) | async-done | bytes 5308432 | tf_op jit(solution)/shard_map/all_gather | solution.py:19
  68.8 5.6 %all-to-all-start = ((bf16[128,8,2592]{0,2,1:T(8,128)(2,1)}), bf16[128,8,2592]{0,2,1:T(8,128)(2,1)}, u32[]{:S(2)}, u32[]{:S(2)}) async-start(bf16[128,8,2592]{0,2,1:T(8,128)(2,1)} %bitcast.72), calls=%async_computation | async-start | bytes 10616832 | tf_op jit(solution)/shard_map/all_to_all | solution.py:20
  74.4 41.4 %all-gather.5.cloned.1.call-done = bf16[1024,1296]{0,1:T(8,128)(2,1)} async-done(((bf16[128,1296]{0,1:T(8,128)(2,1)}), bf16[1024,1296]{0,1:T(8,128)(2,1)}) %all-gather.5.cloned.1.call-update) | async-done | bytes 2654224 | tf_op jit(solution)/shard_map/all_gather | solution.py:23
  119.1 26.5 %all-to-all-done = bf16[128,8,2592]{0,2,1:T(8,128)(2,1)} async-done(((bf16[128,8,2592]{0,2,1:T(8,128)(2,1)}), bf16[128,8,2592]{0,2,1:T(8,128)(2,1)}, u32[]{:S(2)}, u32[]{:S(2)}) %all-to-all-start) | async-done | bytes 5308448 | tf_op jit(solution)/shard_map/all_to_all | solution.py:20
  145.6 13.0 %fusion.2 = f32[1024,1296]{0,1:T(8,128)} fusion(bf16[2592,1296]{0,1:T(8,128)(2,1)} %param.9, bf16[128,8,2592]{0,2,1:T(8,128)(2,1)} %all-to-all-done), kind=kOutput, calls=%fused_computation.2 | convolution fusion | flops 6879707136 | bytes 17335296 | tf_op jit(solution)/shard_map/dot_general | solution.py:21
  158.6 3.5 copy.73
  162.1 3.8 %reshape.45 = bf16[2,144,144,32]{1,0,2,3:T(2,128)(2,1)} reshape(bf16[288,144,32]{0,1,2:T(8,128)(2,1)S(1)} %bitcast.73) | data formatting | bytes 5308416 | tf_op jit(solution)/shard_map/ikac,kcn->ian/dot_general | solution.py:31
  166.0 11.8 %copy.75 = bf16[2,144,144,32]{2,1,3,0:T(8,128)(2,1)} copy(bf16[2,144,144,32]{1,0,2,3:T(2,128)(2,1)} %reshape.45) | data formatting | bytes 5308416 | tf_op jit(solution)/shard_map/ikac,kcn->ian/dot_general | solution.py:31
  177.8 8.0 %copy.72 = bf16[128,20736]{1,0:T(8,128)(2,1)} copy(bf16[128,20736]{0,1:T(8,128)(2,1)} %all-gather.3.cloned.1.call-done) | data formatting | bytes 10616832 | tf_op jit(solution)/shard_map/all_gather | solution.py:19
  185.8 18.4 %reshape.41 = bf16[4,32,144,144,1]{3,2,1,0,4:T(8,128)(2,1)} reshape(bf16[128,20736]{1,0:T(8,128)(2,1)} %copy.72) | data formatting | bytes 10616832 | tf_op jit(solution)/shard_map/reshape | solution.py:29
  204.2 9.0 %fusion.6 = f32[4,144,2,144]{3,1,2,0:T(8,128)S(1)} fusion(bf16[2,144,144,32]{2,1,3,0:T(8,128)(2,1)} %copy.75, bf16[4,32,144,144,1]{3,2,1,0,4:T(8,128)(2,1)} %reshape.41), kind=kOutput, calls=%fused_computation.10 | convolution fusion | flops 1528823808 | bytes 8626176 | tf_op jit(solution)/shard_map/ikac,kcn->ian/dot_general | solution.py:31
  214.2 22.2 %all_to_all.101 = f32[4,144,2,144]{3,2,0,1:T(2,128)S(1)} all-to-all(f32[4,144,2,144]{3,2,0,1:T(2,128)S(1)} %copy.76), channel_id=1, replica_groups=mesh['col'=16,'row'=8] {'col'}, dimensions={1} | all-to-all | bytes 1327104 | tf_op jit(solution)/shard_map/all_to_all | solution.py:33
  237.8 5.8 %all-to-all-start.3 = ((f32[4,9,32,144]{3,0,1,2:T(4,128)}), f32[4,9,32,144]{3,0,1,2:T(4,128)S(1)}, u32[]{:S(2)}, u32[]{:S(2)}) async-start(f32[4,9,32,144]{3,0,1,2:T(4,128)} %bitcast.16), calls=%async_computation.4 | async-start | bytes 2359296 | tf_op jit(solution)/shard_map/all_to_all | solution.py:34
  243.6 16.2 %all-to-all-done.3 = f32[4,9,32,144]{3,0,1,2:T(4,128)S(1)} async-done(((f32[4,9,32,144]{3,0,1,2:T(4,128)}), f32[4,9,32,144]{3,0,1,2:T(4,128)S(1)}, u32[]{:S(2)}, u32[]{:S(2)}) %all-to-all-start.3) | async-done | bytes 663584 | tf_op jit(solution)/shard_map/all_to_all | solution.py:34
  259.8 5.2 %all-to-all-start.1 = ((f32[128,8,128]{2,0,1:T(8,128)}), f32[128,8,128]{2,0,1:T(8,128)}, u32[]{:S(2)}, u32[]{:S(2)}) async-start(f32[128,8,128]{2,0,1:T(8,128)} %all-reduce.2.cloned.1.call-done), calls=%async_computation.2 | async-start | bytes 1048576 | tf_op jit(solution)/shard_map/all_to_all | solution.py:26
  265.3 2.7 copy.83
  267.9 3.9 %reshape.46 = f32[16,1,10368]{2,1,0:T(1,128)} reshape(f32[144,9,4,32]{3,2,1,0:T(4,128)} %bitcast.78) | data formatting | bytes 1327104
  274.2 4.5 %all-to-all-start.4 = ((f32[16,1,10368]{2,1,0:T(1,128)}), f32[16,1,10368]{2,1,0:T(1,128)S(1)}, u32[]{:S(2)}, u32[]{:S(2)}) async-start(f32[16,1,10368]{2,1,0:T(1,128)} %reshape.46), calls=%async_computation.5 | async-start | bytes 1327104 | tf_op jit(solution)/shard_map/all_to_all | solution.py:35
  280.4 2.7 reshape.31
  287.3 3.8 %all-to-all-done.4 = f32[16,1,10368]{2,1,0:T(1,128)S(1)} async-done(((f32[16,1,10368]{2,1,0:T(1,128)}), f32[16,1,10368]{2,1,0:T(1,128)S(1)}, u32[]{:S(2)}, u32[]{:S(2)}) %all-to-all-start.4) | async-done | bytes 663584 | tf_op jit(solution)/shard_map/all_to_all | solution.py:35
  297.0 7.2 %copy.86 = f32[32,144,4,9]{1,3,0,2:T(8,128)} copy(f32[32,144,4,9]{0,2,3,1:T(4,128)} %bitcast.75) | data formatting | bytes 1327104 | tf_op jit(solution)/shard_map/all_to_all | solution.py:35
  307.5 3.5 %reshape.28 = f32[4,32,9,144]{3,2,1,0:T(8,128)} reshape(f32[128,1296]{1,0:T(8,128)} %copy.71) | data formatting | bytes 1327104 | tf_op jit(solution)/shard_map/reshape | solution.py:37
  311.0 3.4 bitcast_divide_fusion
  315.4 22.4 %all_to_all.102 = f32[4,9,32,144]{3,0,1,2:T(4,128)S(1)} all-to-all(f32[4,9,32,144]{3,0,1,2:T(4,128)S(1)} %copy.88), channel_id=1, replica_groups=mesh['col'=16,'row'=8] {'col'}, dimensions={2} | all-to-all | bytes 1327104 | tf_op jit(solution)/shard_map/all_to_all | solution.py:40
  (44 shorter events, 28.9 us)
Async XLA Ops:
  6.5 62.3 %all-gather.3.cloned.1.call-start = ((), (), s32[]{:S(2)}) async-start(), calls=%async_computation.7 | async-start | bytes 5640192 | tf_op jit(solution)/shard_map/all_gather | solution.py:19
  8.4 107.4 %all-gather.5.cloned.1.call-start = ((), (), s32[]{:S(2)}) async-start(), calls=%async_computation.9 | async-start | bytes 2985984 | tf_op jit(solution)/shard_map/all_gather | solution.py:23
  68.8 47.0 %copy-start.3 = (bf16[128,1296]{0,1:T(8,128)(2,1)S(1)}, bf16[128,1296]{0,1:T(8,128)(2,1)}, u32[]{:S(2)}) copy-start(bf16[128,1296]{0,1:T(8,128)(2,1)} %param.8) | copy-start | bytes 995332
  68.8 76.8 %all-to-all-start = ((bf16[128,8,2592]{0,2,1:T(8,128)(2,1)}), bf16[128,8,2592]{0,2,1:T(8,128)(2,1)}, u32[]{:S(2)}, u32[]{:S(2)}) async-start(bf16[128,8,2592]{0,2,1:T(8,128)(2,1)} %bitcast.72), calls=%async_computation | async-start | bytes 10616832 | tf_op jit(solution)/shard_map/all_to_all | solution.py:20
  74.4 169.2 %all-reduce.2.cloned.1.call-start = ((), (), s32[]{:S(2)}) async-start(), calls=%async_computation.10 | async-start | bytes 1048576 | tf_op jit(solution)/shard_map/psum | solution.py:25
  119.0 185.2 %reduce-scatter.2.cloned.1.call-start = ((), (), s32[]{:S(2)}) async-start(), calls=%async_computation.8 | async-start | bytes 5971968 | tf_op jit(solution)/shard_map/reduce_scatter | solution.py:22
  237.8 22.0 %all-to-all-start.3 = ((f32[4,9,32,144]{3,0,1,2:T(4,128)}), f32[4,9,32,144]{3,0,1,2:T(4,128)S(1)}, u32[]{:S(2)}, u32[]{:S(2)}) async-start(f32[4,9,32,144]{3,0,1,2:T(4,128)} %bitcast.16), calls=%async_computation.4 | async-start | bytes 2359296 | tf_op jit(solution)/shard_map/all_to_all | solution.py:34
  259.8 14.5 %all-to-all-start.1 = ((f32[128,8,128]{2,0,1:T(8,128)}), f32[128,8,128]{2,0,1:T(8,128)}, u32[]{:S(2)}, u32[]{:S(2)}) async-start(f32[128,8,128]{2,0,1:T(8,128)} %all-reduce.2.cloned.1.call-done), calls=%async_computation.2 | async-start | bytes 1048576 | tf_op jit(solution)/shard_map/all_to_all | solution.py:26
  267.9 10.8 %copy-start.5 = (u32[128]{0:T(128)S(1)}, u32[128]{0:T(128)}, u32[]{:S(2)}) copy-start(u32[128]{0:T(128)} %constant.2) | copy-start | bytes 1540
  267.9 12.2 %copy-start.4 = (f32[128,1296]{0,1:T(8,128)S(1)}, f32[128,1296]{0,1:T(8,128)}, u32[]{:S(2)}) copy-start(f32[128,1296]{0,1:T(8,128)} %param.7) | copy-start | bytes 1990660
  274.2 16.9 %all-to-all-start.4 = ((f32[16,1,10368]{2,1,0:T(1,128)}), f32[16,1,10368]{2,1,0:T(1,128)S(1)}, u32[]{:S(2)}, u32[]{:S(2)}) async-start(f32[16,1,10368]{2,1,0:T(1,128)} %reshape.46), calls=%async_computation.5 | async-start | bytes 1327104 | tf_op jit(solution)/shard_map/all_to_all | solution.py:35
  297.0 7.2 %copy-start = (bf16[1024,1296]{0,1:T(8,128)(2,1)S(1)}, bf16[1024,1296]{0,1:T(8,128)(2,1)}, u32[]{:S(2)}) copy-start(bf16[1024,1296]{0,1:T(8,128)(2,1)} %all-gather.5.cloned.1.call-done) | copy-start | bytes 7962628
  306.3 4.7 %copy-start.1 = (f32[32,144,4,9]{1,3,0,2:T(8,128)S(1)}, f32[32,144,4,9]{1,3,0,2:T(8,128)}, u32[]{:S(2)}) copy-start(f32[32,144,4,9]{1,3,0,2:T(8,128)} %copy.86) | copy-start | bytes 1990660
  307.5 3.6 %copy-start.2 = (f32[4,9,16,2,144]{4,0,3,2,1:T(4,128)S(1)}, f32[4,9,16,2,144]{4,0,3,2,1:T(4,128)}, u32[]{:S(2)}) copy-start(f32[4,9,16,2,144]{4,0,3,2,1:T(4,128)} %copy.78) | copy-start | bytes 1990660
Sparse Core Ops, SparseCore 0:
  9.5 59.2 all-gather.2
  70.5 45.2 all-gather.4
  119.1 83.9 all-reduce.1
  205.4 38.9 reduce-scatter.1
where the time goes:
time: 348 us; the launch traced here: 347 us
  waiting for transfers between devices  151 us (43%)
  local copies, waits for them, and re-layouts  79.9 us (23%)
  blocking collectives  44.6 us (13%)
  matrix products  26.5 us (8%)
  starting transfers between devices  21.1 us (6%)
  between operations  14 us (4%)
  other arithmetic  10.3 us (3%)
    all_gather x1, waiting for transfers between devices, local_sweep(): t_rows = lax.all_gather(t_bf, 'col', axis=1, tiled=True)  59.6 us
    all_gather x1, waiting for transfers between devices, local_sweep(): t_cols = lax.all_gather(t_bf, 'row', axis=0, tiled=True)  41.4 us
    all_to_all x1, waiting for transfers between devices, local_sweep(): t_ladder = lax.all_to_all(t_rows, 'row', 1, 0, tiled=True)  26.5 us
    all_to_all x1, blocking collectives, local_sweep(): t_pairs = lax.all_to_all(total_sum, 'col', 2, 1, tiled=True)  22.4 us
    all_to_all x1, blocking collectives, local_sweep(): mixed_entry = lax.all_to_all(r_mixed, 'col', 1, 2, tiled=True)  22.2 us
    reshape x1, local copies, waits for them, and re-layouts, local_sweep(): amp_four = t_rows.reshape(occ_r, n_occ, n_vir, n_vir)  18.4 us
    dot_general x3, local copies, waits for them, and re-layouts, local_sweep(): jnp.einsum('ikac,kcn->ian', amp_four, wr_three, preferred_element_type=jn...  16.5 us
    all_to_all x1, waiting for transfers between devices, local_sweep(): swap_rows = lax.all_to_all(mixed_entry, 'row', 2, 0, tiled=True)  16.2 us
  transfers between devices with their start and end apart: 8, of which 6 were waited for; matrix products, arithmetic and copies ran while one was open for 29% of the time, Pallas kernels for 0%

commit v1 on v0

v1 whole, which is shorter than its diff:
```python
import functools
import jax
import jax.numpy as jnp
from jax import lax
from jax.experimental import pallas as pl
from jax.experimental.pallas import tpu as pltpu
from jax.sharding import PartitionSpec as P

MESH = pl.DeviceIdType.MESH
F32 = jnp.float32
BF16 = jnp.bfloat16
BLK = 128
NK = 32
ROWS, COLS = 8, 16
LANES = 128
K_STEP = 4


def lane_tiles(width):
    return [(t, min(LANES, width - LANES * t)) for t in range(-(-width // LANES))]


def sweep_kernel(
    nv,
    t_ref, d_ref, vo_ref, v_hbm, oo_hbm, w_hbm,
    out_ref,
    tc, tl, vv, wt, w2, oo, vrow,
    xs, xr, xs2, xr2, wp, wtr,
    part, pair, hop, fin,
    tf, acc_t, m_send, m_recv, i_recv, iq,
    base, d_send, d_recv, b_send, b_recv, osc, dmat, acc,
    local_sem, x_ss, x_rs, sib_ss, sib_rs, z_ss, z_rs, y_ss, y_rs, f_ss,
    pair_ss, pair_rs, hop_ss, hop_rs, fin_ss, fin_rs,
    xa_ss, xa_rs, xb_ss, xb_rs, w_ss, w_rs, m_ss, m_rs, i_ss, i_rs, d_ss, d_rs, b_ss, b_rs,
):
    row = lax.axis_index("row")
    col = lax.axis_index("col")
    x, k = row // 2, row % 2
    z, y = col // 4, col % 4
    va = nv // 16
    ab = va * nv
    n_w = 2 * nv
    a2 = 2 * va
    cut = (va + 1) // 2 * nv
    halves = [(0, cut), (cut, ab - cut)]
    hrow = ab // 2
    sib = (col, 2 * x + 1 - k)
    finish = []

    def send(src, dst, ss, rs, dev, cond=None):
        cp = pltpu.make_async_remote_copy(
            src_ref=src, dst_ref=dst, send_sem=ss, recv_sem=rs, device_id=dev, device_id_type=MESH)
        if cond is None:
            cp.start()
            finish.append(cp.wait_send)
        else:
            @pl.when(cond)
            def _():
                cp.start()

            def done():
                @pl.when(cond)
                def _():
                    cp.wait_send()
            finish.append(done)

    def arrive(dst, rs):
        pltpu.make_async_remote_copy(
            src_ref=dst, dst_ref=dst, send_sem=rs, recv_sem=rs, device_id=(col, row), device_id_type=MESH
        ).wait_recv()

    loads = [
        pltpu.make_async_copy(v_hbm, vv, local_sem.at[0]),
        pltpu.make_async_copy(w_hbm, wt, local_sem.at[1]),
        pltpu.make_async_copy(
            oo_hbm.at[pl.ds(pl.multiple_of(row * BLK, BLK), BLK), pl.ds(pl.multiple_of(col // 2 * LANES, LANES), LANES)],
            oo, local_sem.at[2]),
    ]
    for cp in loads:
        cp.start()

    barrier = pltpu.get_barrier_semaphore()
    for dlt in range(1, COLS):
        pl.semaphore_signal(barrier, inc=1, device_id=((col + dlt) % COLS, row), device_id_type=MESH)
    for dlt in range(1, 8):
        pl.semaphore_signal(barrier, inc=1, device_id=(col, (row + dlt) % 8), device_id_type=MESH)
    for r2 in range(ROWS):
        for h in range(2):
            pl.semaphore_signal(barrier, inc=1, device_id=(2 * row + h, r2), device_id_type=MESH)
    for s in (1, 3):
        pl.semaphore_signal(barrier, inc=1, device_id=(4 * z + (y + s) % 4, 2 * x + 1 - k), device_id_type=MESH)

    tc[row] = t_ref[...].astype(BF16)
    pl.semaphore_wait(barrier, 15 + 7 + 16 + 2)

    def xdev(s):
        return (col, 2 * ((x + s) % 4) + k)

    def zdev(s):
        return (4 * ((z + s) % 4) + y, row)

    for h, (r0, rn) in enumerate(halves):
        src = tc.at[row, pl.ds(r0, rn), :]
        send(src, src, x_ss.at[0, h], x_rs.at[3, h], xdev(1))
        send(src, src, x_ss.at[1, h], x_rs.at[1, h], xdev(3))
    send(tc.at[row], tc.at[row], sib_ss.at[0], sib_rs.at[0], sib)

    rel = (z - x + 4) % 4
    root = rel == 0
    kap = y // 2
    order = [0, 2, 1, 3]

    def x_step():
        for off, h, s, slot in ((3, 0, 1, 2), (1, 1, 3, 3)):
            xb = (x + off) % 4
            r0, rn = halves[h]
            piece = tc.at[2 * xb + k, pl.ds(r0, rn), :]
            arrive(piece, x_rs.at[off, h])
            send(piece, piece, x_ss.at[slot, h], x_rs.at[2, h], xdev(s))

    def x_rest(off):
        xb = (x + off) % 4
        todo = {3: (1,), 1: (0,), 2: (0, 1)}[off]
        for h in todo:
            r0, rn = halves[h]
            arrive(tc.at[2 * xb + k, pl.ds(r0, rn), :], x_rs.at[off, h])
        src = tc.at[2 * xb + k]
        send(src, src, sib_ss.at[off], sib_rs.at[off], sib)

    def z_send(o):
        off = order[o]
        xb = (x + off) % 4
        for h, (r0, rn) in enumerate(halves):
            src = tc.at[2 * xb + k, pl.ds(r0, rn), :]
            dst = tc.at[8 + xb, pl.ds(r0, rn), :]
            send(src, dst, z_ss.at[o, h], z_rs.at[o, h], zdev(1), root)
        for h, (r0, rn) in reversed(list(enumerate(halves))):
            src = tc.at[2 * xb + k, pl.ds(r0, rn), :]
            dst = tc.at[8 + xb, pl.ds(r0, rn), :]
            send(src, dst, z_ss.at[o, 2 + h], z_rs.at[o, h], zdev(3), root)

    def z_wait(o):
        off = order[o]
        xb = (x + off) % 4
        for h, (r0, rn) in enumerate(halves):
            dst = tc.at[8 + xb, pl.ds(r0, rn), :]

            @pl.when(rel != 0)
            def _():
                arrive(dst, z_rs.at[o, h])
            near, s = ((1, 1), (3, 3))[h]
            send(dst, dst, z_ss.at[o, 4], z_rs.at[o, h], zdev(s), rel == near)

    def z_step(o):
        z_send(o)
        z_wait(o)

    def both(p, q):
        return q if p is None else jnp.logical_and(p, q)

    sel_root = jnp.where(root, 1, 0)

    def y_step(o, cond=None):
        off = order[o]
        xb = (x + off) % 4
        blk = sel_root * (2 * xb + k) + (1 - sel_root) * (8 + xb)
        lanes = pl.ds(pl.multiple_of(k * LANES, LANES), LANES)
        for h, (r0, rn) in enumerate(halves):
            src = tc.at[blk, pl.ds(r0, rn), :]
            dst = tl.at[xb, pl.ds((y % 2) * ab + r0, rn), lanes]
            for n, s in enumerate((1, 3)):
                send(src, dst, y_ss.at[o, h, n], y_rs.at[o, y % 2, k, h],
                     (4 * z + (y + s) % 4, 2 * x + kap), cond)
            send(src, dst, y_ss.at[o, h, 2], y_rs.at[o, y % 2, k, h], sib, both(cond, kap != k))

        @pl.when(both(cond, kap == k))
        def _():
            tl[xb, pl.ds(pl.multiple_of((y % 2) * ab, 16), ab), lanes] = tc[blk]

    def y_piece(o, s, q, h):
        xb = (x + order[o]) % 4
        r0, rn = halves[h]
        return tl.at[xb, pl.ds(s * ab + r0, rn), pl.ds(pl.multiple_of(q * LANES, LANES), LANES)]

    def y_forward(o):
        for s in range(2):
            dist = (y - (2 * k + s) + 4) % 4
            for q in range(2):
                for near, h, step in ((1, 0, 1), (3, 1, 3)):
                    piece = y_piece(o, s, q, h)

                    @pl.when(dist == near)
                    def _():
                        arrive(piece, y_rs.at[o, s, q, h])
                    send(piece, piece, f_ss.at[o, s, q], y_rs.at[o, s, q, h],
                         (4 * z + (y + step) % 4, row), dist == near)

    def y_rest(o):
        for s in range(2):
            dist = (y - (2 * k + s) + 4) % 4
            for q in range(2):
                for h in range(2):
                    piece = y_piece(o, s, q, h)
                    other = (1, 3)[1 - h]
                    need = jnp.where(dist == other, 1, 0) + jnp.where(dist == 2, 1, 0) + (
                        jnp.where(dist == 0, 1, 0) * jnp.where(k == q, 0, 1))

                    @pl.when(need == 1)
                    def _():
                        arrive(piece, y_rs.at[o, s, q, h])

    def ladder(o):
        off = order[o]
        xb = (x + off) % 4
        prod = jnp.dot(vv[...], tl[xb], preferred_element_type=F32)
        part[o, 0] = prod[:, :LANES]
        part[o, 1] = prod[:, LANES:]
        send(part.at[o, 1 - k], pair.at[o], pair_ss.at[o], pair_rs.at[o], sib)

    def pair_step(o):
        arrive(pair.at[o], pair_rs.at[o])
        part[o, k] = part[o, k] + pair[o]

    def hop_step():
        for n in range(2):
            send(part.at[1, k, pl.ds(n * hrow, hrow), :], hop.at[n], hop_ss.at[n], hop_rs.at[n], xdev(1 + 2 * n))

    def fin_step(o):
        n = o - 2
        arrive(hop.at[n], hop_rs.at[n])
        rows = pl.ds(n * hrow, hrow)
        part[o, k, rows, :] = part[o, k, rows, :] + hop[n]
        send(part.at[o, k], fin.at[n], fin_ss.at[n], fin_rs.at[n], xdev(order[o]))

    def mixed(o):
        off = order[o]
        xb = (x + off) % 4

        def turn(a, carry):
            blk = tl[xb, pl.ds(pl.multiple_of(a * nv, 16), nv), :].astype(F32)
            flip = blk.T
            for t, wd in lane_tiles(nv):
                tf[2 * a + t, :, 0:wd] = flip[:, t * LANES:t * LANES + wd]
            return carry

        lax.fori_loop(0, a2, turn, 0, unroll=2)

        def one(k0, carry):
            prod = 0.0
            for kk in [k0 * K_STEP + n for n in range(K_STEP)]:
                cols = []
                for t, wd in lane_tiles(nv):
                    rows = [tf[2 * a + t, pl.ds(kk, 8, stride=NK), :] for a in range(a2)]
                    cols.append(jnp.concatenate(rows, axis=0)[:, :wd].astype(BF16))
                lhs = jnp.concatenate(cols, axis=1) if len(cols) > 1 else cols[0]
                prod = prod + jnp.dot(
                    lhs, w2[pl.ds(pl.multiple_of(kk * nv, 16), nv), :], preferred_element_type=F32)
            for t, wd in lane_tiles(n_w):
                acc_t[t, :, 0:wd] = acc_t[t, :, 0:wd] + prod[:, t * LANES:t * LANES + wd]
            return carry

        acc_t[...] = jnp.zeros_like(acc_t)
        lax.fori_loop(0, NK // K_STEP, one, 0)
        for q in range(2):
            for ip in range(2):
                for i2 in range(2):
                    for t, wd in lane_tiles(n_w):
                        m_send[o, q, ip, i2 * a2:(i2 + 1) * a2, t * LANES:t * LANES + wd] = acc_t[
                            t, pl.ds(q * 4 + ip * 2 + i2, a2, stride=8), :][:, :wd]
            r2 = 2 * xb + q
            own = r2 == row
            send(m_send.at[o, q], m_recv.at[row], m_ss.at[o, q], m_rs.at[row], (col, r2), jnp.logical_not(own))

            @pl.when(own)
            def _():
                m_recv[row] = m_send[o, q]
            for ip in range(2):
                c2 = 4 * xb + 2 * q + ip
                own = jnp.where(c2 == col, 1, 0) * jnp.where(col // 2 == row, 1, 0) == 1
                src = m_send.at[o, q, ip]
                send(src, i_recv.at[row, col % 2], i_ss.at[o, q, ip], i_rs.at[row, col % 2],
                     (c2, col // 2), jnp.logical_not(own))

                @pl.when(own)
                def _():
                    i_recv[row, col % 2] = m_send[o, q, ip]

    def split_rows(src, dst):
        for c2 in range(COLS):
            for i in range(4):
                for t, wd in lane_tiles(ab):
                    dst[c2, t, 2 * i:2 * i + 2, 0:wd] = src[i * NK + 2 * c2:i * NK + 2 * c2 + 2, t * LANES:t * LANES + wd]

    def exchange(src, dst, ss, rs):
        mine = pl.ds(pl.multiple_of(col * 8, 8), 8)
        for dlt in range(1, COLS):
            c2 = (col + dlt) % COLS
            send(src.at[c2], dst.at[:, mine, :], ss.at[dlt], rs.at[dlt], (c2, row))
        dst[:, mine, :] = src[col]

    def exchange_wait(dst, rs):
        for dlt in range(1, COLS):
            c2 = (col + COLS - dlt) % COLS
            arrive(dst.at[:, pl.ds(pl.multiple_of(c2 * 8, 8), 8), :], rs.at[dlt])

    def regroup(src, emit):
        for i in range(4):
            for jp in range(2):
                tiles = [src[t, pl.ds(2 * i + jp, 16, stride=8), :] for t, wd in lane_tiles(ab)]
                for a in range(va):
                    for t, wd in lane_tiles(nv):
                        first, shift = divmod(a * nv + t * LANES, LANES)
                        take = min(wd, LANES - shift)
                        val = tiles[first][:, shift:shift + take]
                        if take < wd:
                            val = jnp.concatenate([val, tiles[first + 1][:, :wd - take]], axis=1)
                        osc[2 * jp + t, pl.ds(a, 16, stride=va), 0:wd] = val
            cols = [osc[2 * jp + t, :, 0:wd] for jp in range(2) for t, wd in lane_tiles(nv)]
            emit(i, jnp.concatenate(cols, axis=1))

    def transpose_bf(val):
        return val.astype(F32).T.astype(BF16)

    def away(src_row, h):
        return jnp.logical_or(row != src_row, 2 * row + h != col)

    z_send(0)
    y_step(0, root)
    x_step()
    z_wait(0)
    y_step(0, rel != 0)
    x_rest(3)
    x_rest(1)
    x_rest(2)
    z_send(1)
    z_send(2)
    z_send(3)
    loads[1].wait()

    def flip_w(n, carry):
        cols = pl.ds(pl.multiple_of(n * LANES, LANES), LANES)
        w2[cols, :] = transpose_bf(wt[:, cols])
        return carry

    lax.fori_loop(0, NK * nv // LANES, flip_w, 0, unroll=3)
    vrow[...] = transpose_bf(vo_ref[...])
    y_forward(0)
    z_wait(1)
    y_step(1)

    for off in range(4):
        arrive(tc.at[2 * ((x + off) % 4) + 1 - k], sib_rs.at[off])
    for r2 in range(ROWS):
        piece = jnp.dot(vrow[...], tc[r2], preferred_element_type=F32).T
        xs[2 * r2] = piece[0:64]
        xs[2 * r2 + 1] = piece[64:]
    for s in (1, 2, 3):
        z2 = (z + s) % 4
        send(xs.at[pl.ds(4 * z2, 4)], xr.at[s], xa_ss.at[s], xa_rs.at[s], zdev(s))
    y_rest(0)
    loads[0].wait()
    ladder(0)
    z_wait(2)
    y_step(2)
    for s in (1, 2, 3):
        arrive(xr.at[s], xa_rs.at[s])
    xs2[...] = xs[pl.ds(4 * z, 4)] + xr[1] + xr[2] + xr[3]
    for s in (1, 2, 3):
        y2 = (y + s) % 4
        send(xs2.at[y2], xr2.at[s], xb_ss.at[s], xb_rs.at[s], (4 * z + y2, row))
    y_forward(1)
    mixed(0)
    pair_step(0)
    z_wait(3)
    y_step(3)
    y_forward(2)
    y_rest(1)
    ladder(1)

    loads[2].wait()
    for s in (1, 2, 3):
        arrive(xr2.at[s], xb_rs.at[s])
    iq[0:LANES, 0:LANES] = oo[...].astype(F32).T
    half = 64 * (col % 2)
    mine = iq[pl.ds(pl.multiple_of(half, 8), 64), 0:LANES]
    wp[...] = (mine + 0.5 * (xs2[y] + xr2[1] + xr2[2] + xr2[3])).astype(BF16)
    w_rows = pl.ds(pl.multiple_of(half, 16), 64)
    self_w = row == col // 2
    for dlt in range(COLS):
        cond = row != col // 2 if dlt == 0 else None
        send(wp, wtr.at[row, w_rows, :], w_ss.at[dlt], w_rs.at[row, col % 2], ((col + dlt) % COLS, col // 2), cond)

    @pl.when(self_w)
    def _():
        wtr[row, w_rows, :] = wp[...]

    pair_step(1)
    hop_step()
    mixed(1)
    y_forward(3)
    base[...] = d_ref[...].T
    split_rows(base, d_send)
    exchange(d_send, d_recv, d_ss, d_rs)
    y_rest(2)
    ladder(2)
    pair_step(2)
    fin_step(2)
    y_rest(3)
    ladder(3)
    mixed(2)
    pair_step(3)
    fin_step(3)

    for r2 in range(ROWS):
        for h in range(2):
            @pl.when(away(r2, h))
            def _():
                arrive(wtr.at[r2, pl.ds(64 * h, 64), :], w_rs.at[r2, h])
    own = vo_ref[...].astype(F32)
    for r2 in range(ROWS):
        own = own + jnp.dot(tc[r2], transpose_bf(wtr[r2]), preferred_element_type=F32)
    part[0, k] = part[0, k] + own
    mixed(3)

    for n in range(2):
        arrive(fin.at[n], fin_rs.at[n])
    base[...] = (part[0, k] + fin[0] + fin[1]).T
    split_rows(base, b_send)
    exchange(b_send, b_recv, b_ss, b_rs)

    exchange_wait(d_recv, d_rs)

    def emit_d(i, val):
        dmat[i * nv:(i + 1) * nv, :] = val

    regroup(d_recv, emit_d)
    for r2 in range(ROWS):
        @pl.when(r2 != row)
        def _():
            arrive(m_recv.at[r2], m_rs.at[r2])
        for h in range(2):
            @pl.when(away(r2, h))
            def _():
                arrive(i_recv.at[r2, h], i_rs.at[r2, h])
    for c2 in range(2):
        parts = []
        for i2 in range(2):
            for r2 in range(ROWS):
                iq[r2 * a2:(r2 + 1) * a2, 0:n_w] = i_recv[r2, c2, i2 * a2:(i2 + 1) * a2, :]
            parts.append(iq[...].T[0:n_w, 0:nv])
        acc[c2 * n_w:(c2 + 1) * n_w, :] = jnp.concatenate(parts, axis=1)
    for r2 in range(ROWS):
        for ip in range(2):
            for i2 in range(2):
                r0 = (2 * ip + i2) * nv + r2 * a2
                acc[r0:r0 + a2, :] = acc[r0:r0 + a2, :] + m_recv[r2, ip, i2 * a2:(i2 + 1) * a2, :]
    exchange_wait(b_recv, b_rs)

    def emit(i, val):
        rows = slice(i * nv, (i + 1) * nv)
        acc[rows, :] = (acc[rows, :] + val) / dmat[rows, :]

    regroup(b_recv, emit)
    out_ref[...] = acc[...].T
    for fn in finish:
        fn()


def solution(mesh):
    def local(t_blk, d_blk, vo_blk, v_blk, oo, w_blk):
        nv = w_blk.shape[0] // NK
        va = nv // 16
        ab = va * nv
        nt = len(lane_tiles(ab))
        nw = 2 * nv
        a2 = 2 * va
        nwt = len(lane_tiles(nw))
        lanes = LANES
        V = pltpu.VMEM
        S = lambda *s: pltpu.SemaphoreType.DMA(s)
        pad = lambda n: -(-n // lanes) * lanes
        scratch = [
            V((12, ab, BLK), BF16), V((4, 2 * ab, 256), BF16), V((ab, 2 * ab), BF16), V((nw, NK * nv), BF16),
            V((NK * nv, nw), BF16), V((lanes, lanes), BF16), V((lanes, ab), BF16),
            V((COLS, 64, lanes), F32), V((4, 4, 64, lanes), F32), V((4, 64, lanes), F32), V((4, 64, lanes), F32), V((64, lanes), BF16), V((ROWS, lanes, lanes), BF16),
            V((4, 2, ab, lanes), F32), V((4, ab, lanes), F32), V((2, ab // 2, lanes), F32), V((2, ab, lanes), F32),
            V((2 * a2, 256, lanes), F32), V((nwt, 8 * a2, lanes), F32),
            V((4, 2, 2, 2 * a2, nw), F32), V((ROWS, 2, 2 * a2, nw), F32), V((ROWS, 2, 2 * a2, nw), F32),
            V((pad(nv), pad(nw)), F32),
            V((lanes, ab), F32), V((COLS, nt, 8, lanes), F32), V((nt, 128, lanes), F32), V((COLS, nt, 8, lanes), F32), V((nt, 128, lanes), F32),
            V((4, nv, lanes), F32), V((4 * nv, nw), F32), V((4 * nv, nw), F32),
            S(3), S(4, 2), S(4, 2), S(4), S(4), S(4, 5), S(4, 2), S(4, 2, 3), S(4, 2, 2, 2), S(4, 2, 2),
            S(4), S(4), S(2), S(2), S(2), S(2),
            S(4), S(4), S(4), S(4), S(COLS), S(ROWS, 2), S(4, 2), S(8), S(4, 2, 2), S(ROWS, 2), S(COLS), S(COLS), S(COLS), S(COLS),
        ]
        vm = pl.BlockSpec(memory_space=pltpu.VMEM)
        hb = pl.BlockSpec(memory_space=pl.ANY)
        out = pl.pallas_call(
            functools.partial(sweep_kernel, nv),
            out_shape=jax.ShapeDtypeStruct((nw, 4 * nv), F32),
            in_specs=[vm, vm, vm, hb, hb, hb],
            out_specs=vm,
            scratch_shapes=scratch,
            compiler_params=pltpu.CompilerParams(
                collective_id=0, has_side_effects=True, vmem_limit_bytes=64 * 1024 * 1024 - 65536),
        )(t_blk.T, d_blk.T, vo_blk.T, v_blk.T, oo, w_blk.T)
        return out.T

    return jax.shard_map(
        local,
        mesh=mesh,
        in_specs=(P("row", "col"), P("row", "col"), P("row", "col"), P("row", "col"), P(None, None), P(None, "col")),
        out_specs=P("row", "col"),
        check_vma=False,
    )
```

time: 348 us -> 159 us (0.46)
  the two profiles are of different devices: /device:TPU:1 before, /device:TPU:29 now
where the time goes in v1:
time: 159 us
  Pallas kernels  157 us (99%)
  local copies, waits for them, and re-layouts  2.03 us (1%)
    pallas_call x1, Pallas kernels, local(): pl.pallas_call(functools.partial(sweep_kernel, nv), out_shape=jax.ShapeDt...  157 us

profile of v1, /device:TPU:29, one launch (start us, length us, event | category | flops | bytes accessed | tf_op | source)
XLA Modules:
  0.0 158.6 jit_solution(4577304509886524045)
XLA Ops:
  0.0 156.6 %shard_map.64 = f32[288,576]{1,0:T(8,128)} custom-call(f32[1296,128]{1,0:T(8,128)} %bitcast.9, f32[1296,128]{1,0:T(8,128)} %bitcast.10, bf16[1296,128]{1,0:T(8,128)(2,1)} %bitcast.11, bf16[1296,2592]{1,0:T(8,128)(2,1)} %bitcast.6, bf16[1024,1024]{1,0:T(8,128)(2,1)} %oo_hbm.1, bf16[288,4608]{1,0:T(8,128)(2,1)} %bitcast.8), custom_call_target="tpu_custom_call" | custom-call | tf_op jit(solution)/shard_map/pallas_call | solution.py:498
  156.6 2.0 %copy.8 = f32[576,288]{0,1:T(8,128)} copy(f32[576,288]{0,1:T(8,128)} %bitcast.7) | data formatting | bytes 1327104

commit v2 on v1

--- a/solution.py
+++ b/solution.py
@@ -20,6 +20,10 @@
     return [(t, min(LANES, width - LANES * t)) for t in range(-(-width // LANES))]
 
 
+def dot_nt(lhs, rhs):
+    return lax.dot_general(lhs, rhs, (((1,), (1,)), ((), ())), preferred_element_type=F32)
+
+
 def sweep_kernel(
     nv,
     t_ref, d_ref, vo_ref, v_hbm, oo_hbm, w_hbm,
@@ -27,11 +31,11 @@
     tc, tl, vv, wt, w2, oo, vrow,
     xs, xr, xs2, xr2, wp, wtr,
     part, pair, hop, fin,
-    tf, acc_t, m_send, m_recv, i_recv, iq,
+    tf, acc_t, perm, near, m_send, m_recv, i_recv, iq,
     base, d_send, d_recv, b_send, b_recv, osc, dmat, acc,
     local_sem, x_ss, x_rs, sib_ss, sib_rs, z_ss, z_rs, y_ss, y_rs, f_ss,
     pair_ss, pair_rs, hop_ss, hop_rs, fin_ss, fin_rs,
-    xa_ss, xa_rs, xb_ss, xb_rs, w_ss, w_rs, m_ss, m_rs, i_ss, i_rs, d_ss, d_rs, b_ss, b_rs,
+    xa_ss, xa_rs, xb_ss, xb_rs, w_ss, w_rs, m_ss, m_rs, n_ss, n_rs, i_ss, i_rs, d_ss, d_rs, b_ss, b_rs,
 ):
     row = lax.axis_index("row")
     col = lax.axis_index("col")
@@ -70,12 +74,14 @@
         ).wait_recv()
 
     loads = [
-        pltpu.make_async_copy(v_hbm, vv, local_sem.at[0]),
+        pltpu.make_async_copy(v_hbm.at[pl.ds(0, hrow)], vv.at[0], local_sem.at[0]),
+        pltpu.make_async_copy(v_hbm.at[pl.ds(hrow, hrow)], vv.at[1], local_sem.at[3]),
         pltpu.make_async_copy(w_hbm, wt, local_sem.at[1]),
         pltpu.make_async_copy(
             oo_hbm.at[pl.ds(pl.multiple_of(row * BLK, BLK), BLK), pl.ds(pl.multiple_of(col // 2 * LANES, LANES), LANES)],
             oo, local_sem.at[2]),
     ]
+    load_v, load_v2, load_w, load_oo = loads
     for cp in loads:
         cp.start()
 
@@ -99,10 +105,15 @@
     def zdev(s):
         return (4 * ((z + s) % 4) + y, row)
 
-    for h, (r0, rn) in enumerate(halves):
-        src = tc.at[row, pl.ds(r0, rn), :]
+    def piece_of(blk, h):
+        r0, rn = halves[h]
+        return tc.at[blk, pl.ds(r0, rn), :]
+
+    for h in range(2):
+        src = piece_of(row, h)
         send(src, src, x_ss.at[0, h], x_rs.at[3, h], xdev(1))
-        send(src, src, x_ss.at[1, h], x_rs.at[1, h], xdev(3))
+        src = piece_of(row, 1 - h)
+        send(src, src, x_ss.at[1, 1 - h], x_rs.at[1, 1 - h], xdev(3))
     send(tc.at[row], tc.at[row], sib_ss.at[0], sib_rs.at[0], sib)
 
     rel = (z - x + 4) % 4
@@ -148,8 +159,8 @@
             @pl.when(rel != 0)
             def _():
                 arrive(dst, z_rs.at[o, h])
-            near, s = ((1, 1), (3, 3))[h]
-            send(dst, dst, z_ss.at[o, 4], z_rs.at[o, h], zdev(s), rel == near)
+            step = (1, 3)[h]
+            send(dst, dst, z_ss.at[o, 4], z_rs.at[o, h], zdev(step), rel == step)
 
     def z_step(o):
         z_send(o)
@@ -166,11 +177,15 @@
         blk = sel_root * (2 * xb + k) + (1 - sel_root) * (8 + xb)
         lanes = pl.ds(pl.multiple_of(k * LANES, LANES), LANES)
         for h, (r0, rn) in enumerate(halves):
-            src = tc.at[blk, pl.ds(r0, rn), :]
+            for n, s in enumerate((1, 3)):
+                g = abs(n - h)
+                src = piece_of(blk, g)
+                dst = tl.at[xb, pl.ds((y % 2) * ab + halves[g][0], halves[g][1]), lanes]
+                send(src, dst, y_ss.at[o, g, n], y_rs.at[o, y % 2, k, g],
+                     (4 * z + (y + s) % 4, 2 * x + kap), cond)
+        for h, (r0, rn) in enumerate(halves):
+            src = piece_of(blk, h)
             dst = tl.at[xb, pl.ds((y % 2) * ab + r0, rn), lanes]
-            for n, s in enumerate((1, 3)):
-                send(src, dst, y_ss.at[o, h, n], y_rs.at[o, y % 2, k, h],
-                     (4 * z + (y + s) % 4, 2 * x + kap), cond)
             send(src, dst, y_ss.at[o, h, 2], y_rs.at[o, y % 2, k, h], sib, both(cond, kap != k))
 
         @pl.when(both(cond, kap == k))
@@ -186,14 +201,14 @@
         for s in range(2):
             dist = (y - (2 * k + s) + 4) % 4
             for q in range(2):
-                for near, h, step in ((1, 0, 1), (3, 1, 3)):
+                for h, step in ((0, 1), (1, 3)):
                     piece = y_piece(o, s, q, h)
 
-                    @pl.when(dist == near)
+                    @pl.when(dist == step)
                     def _():
                         arrive(piece, y_rs.at[o, s, q, h])
                     send(piece, piece, f_ss.at[o, s, q], y_rs.at[o, s, q, h],
-                         (4 * z + (y + step) % 4, row), dist == near)
+                         (4 * z + (y + step) % 4, row), dist == step)
 
     def y_rest(o):
         for s in range(2):
@@ -212,9 +227,15 @@
     def ladder(o):
         off = order[o]
         xb = (x + off) % 4
-        prod = jnp.dot(vv[...], tl[xb], preferred_element_type=F32)
-        part[o, 0] = prod[:, :LANES]
-        part[o, 1] = prod[:, LANES:]
+
+        def some_rows(n, carry):
+            rows = pl.ds(pl.multiple_of(n * hrow, 8), hrow)
+            prod = jnp.dot(vv[n], tl[xb], preferred_element_type=F32)
+            part[o, 0, rows, :] = prod[:, :LANES]
+            part[o, 1, rows, :] = prod[:, LANES:]
+            return carry
+
+        lax.fori_loop(0, 2, some_rows, 0)
         send(part.at[o, 1 - k], pair.at[o], pair_ss.at[o], pair_rs.at[o], sib)
 
     def pair_step(o):
@@ -237,8 +258,8 @@
         xb = (x + off) % 4
 
         def turn(a, carry):
-            blk = tl[xb, pl.ds(pl.multiple_of(a * nv, 16), nv), :].astype(F32)
-            flip = blk.T
+            blk = tl[xb, pl.ds(pl.multiple_of(a * nv, 16), nv), :]
+            flip = dot_nt(perm[...], blk)
             for t, wd in lane_tiles(nv):
                 tf[2 * a + t, :, 0:wd] = flip[:, t * LANES:t * LANES + wd]
             return carry
@@ -250,7 +271,7 @@
             for kk in [k0 * K_STEP + n for n in range(K_STEP)]:
                 cols = []
                 for t, wd in lane_tiles(nv):
-                    rows = [tf[2 * a + t, pl.ds(kk, 8, stride=NK), :] for a in range(a2)]
+                    rows = [tf[2 * a + t, pl.ds(pl.multiple_of(kk * 8, 8), 8), :] for a in range(a2)]
                     cols.append(jnp.concatenate(rows, axis=0)[:, :wd].astype(BF16))
                 lhs = jnp.concatenate(cols, axis=1) if len(cols) > 1 else cols[0]
                 prod = prod + jnp.dot(
@@ -274,16 +295,31 @@
             @pl.when(own)
             def _():
                 m_recv[row] = m_send[o, q]
+
+    def image_near(o):
+        for q in range(2):
             for ip in range(2):
-                c2 = 4 * xb + 2 * q + ip
-                own = jnp.where(c2 == col, 1, 0) * jnp.where(col // 2 == row, 1, 0) == 1
+                c2 = 4 * ((x + order[o]) % 4) + 2 * q + ip
+                own = c2 == col
                 src = m_send.at[o, q, ip]
-                send(src, i_recv.at[row, col % 2], i_ss.at[o, q, ip], i_rs.at[row, col % 2],
-                     (c2, col // 2), jnp.logical_not(own))
+                send(src, near.at[col], n_ss.at[o, q, ip], n_rs.at[col], (c2, row), jnp.logical_not(own))
 
                 @pl.when(own)
                 def _():
-                    i_recv[row, col % 2] = m_send[o, q, ip]
+                    near[col] = m_send[o, q, ip]
+
+    def image_far():
+        for r2 in range(ROWS):
+            for c2 in (2 * r2, 2 * r2 + 1):
+                @pl.when(col != c2)
+                def _():
+                    arrive(near.at[c2], n_rs.at[c2])
+            own = row == r2
+            send(near.at[pl.ds(2 * r2, 2)], i_recv.at[row], i_ss.at[r2], i_rs.at[row], (col, r2), jnp.logical_not(own))
+
+            @pl.when(own)
+            def _():
+                i_recv[row] = near[pl.ds(2 * r2, 2)]
 
     def split_rows(src, dst):
         for c2 in range(COLS):
@@ -329,13 +365,11 @@
     x_step()
     z_wait(0)
     y_step(0, rel != 0)
-    x_rest(3)
-    x_rest(1)
-    x_rest(2)
-    z_send(1)
-    z_send(2)
-    z_send(3)
-    loads[1].wait()
+    for off in (3, 1, 2):
+        x_rest(off)
+    for o in (1, 2, 3):
+        z_send(o)
+    load_w.wait()
 
     def flip_w(n, carry):
         cols = pl.ds(pl.multiple_of(n * LANES, LANES), LANES)
@@ -344,6 +378,9 @@
 
     lax.fori_loop(0, NK * nv // LANES, flip_w, 0, unroll=3)
     vrow[...] = transpose_bf(vo_ref[...])
+    r_id = lax.broadcasted_iota(jnp.int32, perm.shape, 0)
+    c_id = lax.broadcasted_iota(jnp.int32, perm.shape, 1)
+    perm[...] = jnp.where((r_id % 8) * NK + r_id // 8 == c_id, 1.0, 0.0).astype(BF16)
     y_forward(0)
     z_wait(1)
     y_step(1)
@@ -358,16 +395,11 @@
         z2 = (z + s) % 4
         send(xs.at[pl.ds(4 * z2, 4)], xr.at[s], xa_ss.at[s], xa_rs.at[s], zdev(s))
     y_rest(0)
-    loads[0].wait()
+    load_v.wait()
+    load_v2.wait()
     ladder(0)
     z_wait(2)
     y_step(2)
-    for s in (1, 2, 3):
-        arrive(xr.at[s], xa_rs.at[s])
-    xs2[...] = xs[pl.ds(4 * z, 4)] + xr[1] + xr[2] + xr[3]
-    for s in (1, 2, 3):
-        y2 = (y + s) % 4
-        send(xs2.at[y2], xr2.at[s], xb_ss.at[s], xb_rs.at[s], (4 * z + y2, row))
     y_forward(1)
     mixed(0)
     pair_step(0)
@@ -376,8 +408,19 @@
     y_forward(2)
     y_rest(1)
     ladder(1)
-
-    loads[2].wait()
+    for s in (1, 2, 3):
+        arrive(xr.at[s], xa_rs.at[s])
+    xs2[...] = xs[pl.ds(4 * z, 4)] + xr[1] + xr[2] + xr[3]
+    for s in (1, 2, 3):
+        y2 = (y + s) % 4
+        send(xs2.at[y2], xr2.at[s], xb_ss.at[s], xb_rs.at[s], (4 * z + y2, row))
+    y_forward(3)
+    pair_step(1)
+    hop_step()
+    y_rest(2)
+    ladder(2)
+
+    load_oo.wait()
     for s in (1, 2, 3):
         arrive(xr2.at[s], xb_rs.at[s])
     iq[0:LANES, 0:LANES] = oo[...].astype(F32).T
@@ -385,31 +428,30 @@
     mine = iq[pl.ds(pl.multiple_of(half, 8), 64), 0:LANES]
     wp[...] = (mine + 0.5 * (xs2[y] + xr2[1] + xr2[2] + xr2[3])).astype(BF16)
     w_rows = pl.ds(pl.multiple_of(half, 16), 64)
-    self_w = row == col // 2
     for dlt in range(COLS):
         cond = row != col // 2 if dlt == 0 else None
         send(wp, wtr.at[row, w_rows, :], w_ss.at[dlt], w_rs.at[row, col % 2], ((col + dlt) % COLS, col // 2), cond)
 
-    @pl.when(self_w)
+    @pl.when(row == col // 2)
     def _():
         wtr[row, w_rows, :] = wp[...]
 
-    pair_step(1)
-    hop_step()
+    image_near(0)
     mixed(1)
-    y_forward(3)
+    image_near(1)
+    y_rest(3)
+    ladder(3)
+    pair_step(2)
+    fin_step(2)
     base[...] = d_ref[...].T
     split_rows(base, d_send)
     exchange(d_send, d_recv, d_ss, d_rs)
-    y_rest(2)
-    ladder(2)
-    pair_step(2)
-    fin_step(2)
-    y_rest(3)
-    ladder(3)
-    mixed(2)
     pair_step(3)
     fin_step(3)
+    mixed(2)
+    image_near(2)
+    mixed(3)
+    image_near(3)
 
     for r2 in range(ROWS):
         for h in range(2):
@@ -420,7 +462,7 @@
     for r2 in range(ROWS):
         own = own + jnp.dot(tc[r2], transpose_bf(wtr[r2]), preferred_element_type=F32)
     part[0, k] = part[0, k] + own
-    mixed(3)
+    image_far()
 
     for n in range(2):
         arrive(fin.at[n], fin_rs.at[n])
@@ -438,10 +480,7 @@
         @pl.when(r2 != row)
         def _():
             arrive(m_recv.at[r2], m_rs.at[r2])
-        for h in range(2):
-            @pl.when(away(r2, h))
-            def _():
-                arrive(i_recv.at[r2, h], i_rs.at[r2, h])
+            arrive(i_recv.at[r2], i_rs.at[r2])
     for c2 in range(2):
         parts = []
         for i2 in range(2):
@@ -480,18 +519,18 @@
         S = lambda *s: pltpu.SemaphoreType.DMA(s)
         pad = lambda n: -(-n // lanes) * lanes
         scratch = [
-            V((12, ab, BLK), BF16), V((4, 2 * ab, 256), BF16), V((ab, 2 * ab), BF16), V((nw, NK * nv), BF16),
+            V((12, ab, BLK), BF16), V((4, 2 * ab, 256), BF16), V((2, ab // 2, 2 * ab), BF16), V((nw, NK * nv), BF16),
             V((NK * nv, nw), BF16), V((lanes, lanes), BF16), V((lanes, ab), BF16),
             V((COLS, 64, lanes), F32), V((4, 4, 64, lanes), F32), V((4, 64, lanes), F32), V((4, 64, lanes), F32), V((64, lanes), BF16), V((ROWS, lanes, lanes), BF16),
             V((4, 2, ab, lanes), F32), V((4, ab, lanes), F32), V((2, ab // 2, lanes), F32), V((2, ab, lanes), F32),
             V((2 * a2, 256, lanes), F32), V((nwt, 8 * a2, lanes), F32),
-            V((4, 2, 2, 2 * a2, nw), F32), V((ROWS, 2, 2 * a2, nw), F32), V((ROWS, 2, 2 * a2, nw), F32),
+            V((256, 256), BF16), V((COLS, 2 * a2, nw), F32), V((4, 2, 2, 2 * a2, nw), F32), V((ROWS, 2, 2 * a2, nw), F32), V((ROWS, 2, 2 * a2, nw), F32),
             V((pad(nv), pad(nw)), F32),
             V((lanes, ab), F32), V((COLS, nt, 8, lanes), F32), V((nt, 128, lanes), F32), V((COLS, nt, 8, lanes), F32), V((nt, 128, lanes), F32),
             V((4, nv, lanes), F32), V((4 * nv, nw), F32), V((4 * nv, nw), F32),
-            S(3), S(4, 2), S(4, 2), S(4), S(4), S(4, 5), S(4, 2), S(4, 2, 3), S(4, 2, 2, 2), S(4, 2, 2),
+            S(4), S(4, 2), S(4, 2), S(4), S(4), S(4, 5), S(4, 2), S(4, 2, 3), S(4, 2, 2, 2), S(4, 2, 2),
             S(4), S(4), S(2), S(2), S(2), S(2),
-            S(4), S(4), S(4), S(4), S(COLS), S(ROWS, 2), S(4, 2), S(8), S(4, 2, 2), S(ROWS, 2), S(COLS), S(COLS), S(COLS), S(COLS),
+            S(4), S(4), S(4), S(4), S(COLS), S(ROWS, 2), S(4, 2), S(8), S(4, 2, 2), S(COLS), S(ROWS), S(ROWS), S(COLS), S(COLS), S(COLS), S(COLS),
         ]
         vm = pl.BlockSpec(memory_space=pltpu.VMEM)
         hb = pl.BlockSpec(memory_space=pl.ANY)

time: 159 us -> 124 us (0.78)
  the two profiles are of different devices: /device:TPU:29 before, /device:TPU:1 now
where the time goes in v2:
time: 124 us
  Pallas kernels  122 us (98%)
  local copies, waits for them, and re-layouts  2.03 us (2%)
    pallas_call x1, Pallas kernels, local(): pl.pallas_call(functools.partial(sweep_kernel, nv), out_shape=jax.ShapeDt...  122 us

profile of v2, /device:TPU:1, one launch (start us, length us, event | category | flops | bytes accessed | tf_op | source)
XLA Modules:
  0.0 123.9 jit_solution(9206021853579997955)
XLA Ops:
  0.0 121.9 %shard_map.64 = f32[288,576]{1,0:T(8,128)} custom-call(f32[1296,128]{1,0:T(8,128)} %bitcast.9, f32[1296,128]{1,0:T(8,128)} %bitcast.10, bf16[1296,128]{1,0:T(8,128)(2,1)} %bitcast.11, bf16[1296,2592]{1,0:T(8,128)(2,1)} %bitcast.6, bf16[1024,1024]{1,0:T(8,128)(2,1)} %oo_hbm.1, bf16[288,4608]{1,0:T(8,128)(2,1)} %bitcast.8), custom_call_target="tpu_custom_call" | custom-call | tf_op jit(solution)/shard_map/pallas_call | solution.py:537
  121.9 2.0 %copy.8 = f32[576,288]{0,1:T(8,128)} copy(f32[576,288]{0,1:T(8,128)} %bitcast.7) | data formatting | bytes 1327104

commit v3 on v2

--- a/solution.py
+++ b/solution.py
@@ -12,6 +12,7 @@
 BLK = 128
 NK = 32
 ROWS, COLS = 8, 16
+OTHERS = (1, 2, 3)
 LANES = 128
 K_STEP = 4
 
@@ -20,16 +21,29 @@
     return [(t, min(LANES, width - LANES * t)) for t in range(-(-width // LANES))]
 
 
+def piece_parts(nv, t, width, i2):
+    a2 = nv // 8
+    tall = -(-2 * a2 // 8) * 8
+    if 4 * width > LANES:
+        return [(t * tall + i2 * a2, a2, 0, 0)]
+    return [(t * tall, a2 // 2, (2 * i2 + g) * width, g * (a2 // 2)) for g in range(2)]
+
+
+def piece_rows(nv):
+    a2 = nv // 8
+    return sum(-(-(a2 // 2 if 4 * wd <= LANES else 2 * a2) // 8) * 8 for t, wd in lane_tiles(2 * nv))
+
+
 def dot_nt(lhs, rhs):
     return lax.dot_general(lhs, rhs, (((1,), (1,)), ((), ())), preferred_element_type=F32)
 
 
 def sweep_kernel(
     nv,
-    t_ref, d_ref, vo_ref, v_hbm, oo_hbm, w_hbm,
-    out_ref,
+    t_ref, d_hbm, vo_hbm, v_hbm, oo_hbm, w_hbm,
+    out_ref, d_ref, vo_ref,
     tc, tl, vv, wt, w2, oo, vrow,
-    xs, xr, xs2, xr2, wp, wtr,
+    known, xs, xr, xs2, xr2, wp, wtr,
     part, pair, hop, fin,
     tf, acc_t, perm, near, m_send, m_recv, i_recv, iq,
     base, d_send, d_recv, b_send, b_recv, osc, dmat, acc,
@@ -81,29 +95,34 @@
             oo_hbm.at[pl.ds(pl.multiple_of(row * BLK, BLK), BLK), pl.ds(pl.multiple_of(col // 2 * LANES, LANES), LANES)],
             oo, local_sem.at[2]),
     ]
-    load_v, load_v2, load_w, load_oo = loads
+    loads += [pltpu.make_async_copy(vo_hbm, vo_ref, local_sem.at[4]), pltpu.make_async_copy(d_hbm, d_ref, local_sem.at[5])]
+    load_v, load_v2, load_w, load_oo, load_vo, load_d = loads
     for cp in loads:
         cp.start()
 
-    barrier = pltpu.get_barrier_semaphore()
-    for dlt in range(1, COLS):
-        pl.semaphore_signal(barrier, inc=1, device_id=((col + dlt) % COLS, row), device_id_type=MESH)
-    for dlt in range(1, 8):
-        pl.semaphore_signal(barrier, inc=1, device_id=(col, (row + dlt) % 8), device_id_type=MESH)
-    for r2 in range(ROWS):
-        for h in range(2):
-            pl.semaphore_signal(barrier, inc=1, device_id=(2 * row + h, r2), device_id_type=MESH)
-    for s in (1, 3):
-        pl.semaphore_signal(barrier, inc=1, device_id=(4 * z + (y + s) % 4, 2 * x + 1 - k), device_id_type=MESH)
-
-    tc[row] = t_ref[...].astype(BF16)
-    pl.semaphore_wait(barrier, 15 + 7 + 16 + 2)
-
     def xdev(s):
         return (col, 2 * ((x + s) % 4) + k)
 
     def zdev(s):
         return (4 * ((z + s) % 4) + y, row)
+
+    def ydev(s, core):
+        return (4 * z + (y + s) % 4, 2 * x + core)
+
+    next_to = [sib] + [f(s) for f in (xdev, zdev) for s in (1, 3)] + [ydev(s, c) for s in (1, 3) for c in (k, 1 - k)]
+    barrier = pltpu.get_barrier_semaphore()
+    for dev in next_to:
+        pl.semaphore_signal(barrier, inc=1, device_id=dev, device_id_type=MESH)
+
+    def hello(n):
+        for dev in next_to:
+            pl.semaphore_signal(known.at[n], inc=1, device_id=dev, device_id_type=MESH)
+
+    def heard(n):
+        pl.semaphore_wait(known.at[n], len(next_to))
+
+    tc[row] = t_ref[...].astype(BF16)
+    pl.semaphore_wait(barrier, len(next_to))
 
     def piece_of(blk, h):
         r0, rn = halves[h]
@@ -286,8 +305,13 @@
             for ip in range(2):
                 for i2 in range(2):
                     for t, wd in lane_tiles(n_w):
-                        m_send[o, q, ip, i2 * a2:(i2 + 1) * a2, t * LANES:t * LANES + wd] = acc_t[
-                            t, pl.ds(q * 4 + ip * 2 + i2, a2, stride=8), :][:, :wd]
+                        val = acc_t[t, pl.ds(q * 4 + ip * 2 + i2, a2, stride=8), :][:, :wd]
+                        for r0, rn, c0, v0 in piece_parts(nv, t, wd, i2):
+                            m_send[o, q, ip, r0:r0 + rn, c0:c0 + wd] = val[v0:v0 + rn]
+
+    def mixed_far(o):
+        xb = (x + order[o]) % 4
+        for q in range(2):
             r2 = 2 * xb + q
             own = r2 == row
             send(m_send.at[o, q], m_recv.at[row], m_ss.at[o, q], m_rs.at[row], (col, r2), jnp.logical_not(own))
@@ -295,6 +319,13 @@
             @pl.when(own)
             def _():
                 m_recv[row] = m_send[o, q]
+
+    def unpack(src, i2):
+        cols = []
+        for t, wd in lane_tiles(n_w):
+            rows = [src[r0:r0 + rn, c0:c0 + wd] for r0, rn, c0, v0 in piece_parts(nv, t, wd, i2)]
+            cols.append(jnp.concatenate(rows, axis=0) if len(rows) > 1 else rows[0])
+        return jnp.concatenate(cols, axis=1) if len(cols) > 1 else cols[0]
 
     def image_near(o):
         for q in range(2):
@@ -362,13 +393,18 @@
 
     z_send(0)
     y_step(0, root)
+    hello(0)
     x_step()
     z_wait(0)
     y_step(0, rel != 0)
+    heard(0)
+    hello(1)
     for off in (3, 1, 2):
         x_rest(off)
-    for o in (1, 2, 3):
+    for o in OTHERS:
         z_send(o)
+    heard(1)
+    hello(2)
     load_w.wait()
 
     def flip_w(n, carry):
@@ -377,10 +413,13 @@
         return carry
 
     lax.fori_loop(0, NK * nv // LANES, flip_w, 0, unroll=3)
+    load_vo.wait()
     vrow[...] = transpose_bf(vo_ref[...])
     r_id = lax.broadcasted_iota(jnp.int32, perm.shape, 0)
     c_id = lax.broadcasted_iota(jnp.int32, perm.shape, 1)
     perm[...] = jnp.where((r_id % 8) * NK + r_id // 8 == c_id, 1.0, 0.0).astype(BF16)
+    heard(2)
+    hello(3)
     y_forward(0)
     z_wait(1)
     y_step(1)
@@ -391,7 +430,7 @@
         piece = jnp.dot(vrow[...], tc[r2], preferred_element_type=F32).T
         xs[2 * r2] = piece[0:64]
         xs[2 * r2 + 1] = piece[64:]
-    for s in (1, 2, 3):
+    for s in OTHERS:
         z2 = (z + s) % 4
         send(xs.at[pl.ds(4 * z2, 4)], xr.at[s], xa_ss.at[s], xa_rs.at[s], zdev(s))
     y_rest(0)
@@ -400,28 +439,34 @@
     ladder(0)
     z_wait(2)
     y_step(2)
+    heard(3)
+    hello(4)
     y_forward(1)
     mixed(0)
+    mixed_far(0)
     pair_step(0)
     z_wait(3)
     y_step(3)
     y_forward(2)
     y_rest(1)
     ladder(1)
-    for s in (1, 2, 3):
+    for s in OTHERS:
         arrive(xr.at[s], xa_rs.at[s])
     xs2[...] = xs[pl.ds(4 * z, 4)] + xr[1] + xr[2] + xr[3]
-    for s in (1, 2, 3):
+    for s in OTHERS:
         y2 = (y + s) % 4
         send(xs2.at[y2], xr2.at[s], xb_ss.at[s], xb_rs.at[s], (4 * z + y2, row))
-    y_forward(3)
+    mixed(1)
     pair_step(1)
     hop_step()
+    mixed_far(1)
+    y_forward(3)
     y_rest(2)
     ladder(2)
 
     load_oo.wait()
-    for s in (1, 2, 3):
+    heard(4)
+    for s in OTHERS:
         arrive(xr2.at[s], xb_rs.at[s])
     iq[0:LANES, 0:LANES] = oo[...].astype(F32).T
     half = 64 * (col % 2)
@@ -437,12 +482,12 @@
         wtr[row, w_rows, :] = wp[...]
 
     image_near(0)
-    mixed(1)
     image_near(1)
     y_rest(3)
     ladder(3)
     pair_step(2)
     fin_step(2)
+    load_d.wait()
     base[...] = d_ref[...].T
     split_rows(base, d_send)
     exchange(d_send, d_recv, d_ss, d_rs)
@@ -450,8 +495,10 @@
     fin_step(3)
     mixed(2)
     image_near(2)
+    mixed_far(2)
     mixed(3)
     image_near(3)
+    mixed_far(3)
 
     for r2 in range(ROWS):
         for h in range(2):
@@ -480,19 +527,22 @@
         @pl.when(r2 != row)
         def _():
             arrive(m_recv.at[r2], m_rs.at[r2])
+        for ip in range(2):
+            for i2 in range(2):
+                r0 = (2 * ip + i2) * nv + r2 * a2
+                acc[r0:r0 + a2, :] = unpack(m_recv.at[r2, ip], i2)
+    for r2 in range(ROWS):
+        @pl.when(r2 != row)
+        def _():
             arrive(i_recv.at[r2], i_rs.at[r2])
     for c2 in range(2):
         parts = []
         for i2 in range(2):
             for r2 in range(ROWS):
-                iq[r2 * a2:(r2 + 1) * a2, 0:n_w] = i_recv[r2, c2, i2 * a2:(i2 + 1) * a2, :]
+                iq[r2 * a2:(r2 + 1) * a2, 0:n_w] = unpack(i_recv.at[r2, c2], i2)
             parts.append(iq[...].T[0:n_w, 0:nv])
-        acc[c2 * n_w:(c2 + 1) * n_w, :] = jnp.concatenate(parts, axis=1)
-    for r2 in range(ROWS):
-        for ip in range(2):
-            for i2 in range(2):
-                r0 = (2 * ip + i2) * nv + r2 * a2
-                acc[r0:r0 + a2, :] = acc[r0:r0 + a2, :] + m_recv[r2, ip, i2 * a2:(i2 + 1) * a2, :]
+        rows = slice(c2 * n_w, (c2 + 1) * n_w)
+        acc[rows, :] = acc[rows, :] + jnp.concatenate(parts, axis=1)
     exchange_wait(b_recv, b_rs)
 
     def emit(i, val):
@@ -514,21 +564,23 @@
         nw = 2 * nv
         a2 = 2 * va
         nwt = len(lane_tiles(nw))
+        pr = piece_rows(nv)
         lanes = LANES
         V = pltpu.VMEM
         S = lambda *s: pltpu.SemaphoreType.DMA(s)
         pad = lambda n: -(-n // lanes) * lanes
         scratch = [
+            V((ab, BLK), F32), V((ab, BLK), BF16),
             V((12, ab, BLK), BF16), V((4, 2 * ab, 256), BF16), V((2, ab // 2, 2 * ab), BF16), V((nw, NK * nv), BF16),
             V((NK * nv, nw), BF16), V((lanes, lanes), BF16), V((lanes, ab), BF16),
-            V((COLS, 64, lanes), F32), V((4, 4, 64, lanes), F32), V((4, 64, lanes), F32), V((4, 64, lanes), F32), V((64, lanes), BF16), V((ROWS, lanes, lanes), BF16),
+            pltpu.SemaphoreType.REGULAR((5,)), V((COLS, 64, lanes), F32), V((4, 4, 64, lanes), F32), V((4, 64, lanes), F32), V((4, 64, lanes), F32), V((64, lanes), BF16), V((ROWS, lanes, lanes), BF16),
             V((4, 2, ab, lanes), F32), V((4, ab, lanes), F32), V((2, ab // 2, lanes), F32), V((2, ab, lanes), F32),
             V((2 * a2, 256, lanes), F32), V((nwt, 8 * a2, lanes), F32),
-            V((256, 256), BF16), V((COLS, 2 * a2, nw), F32), V((4, 2, 2, 2 * a2, nw), F32), V((ROWS, 2, 2 * a2, nw), F32), V((ROWS, 2, 2 * a2, nw), F32),
+            V((256, 256), BF16), V((COLS, pr, lanes), F32), V((4, 2, 2, pr, lanes), F32), V((ROWS, 2, pr, lanes), F32), V((ROWS, 2, pr, lanes), F32),
             V((pad(nv), pad(nw)), F32),
             V((lanes, ab), F32), V((COLS, nt, 8, lanes), F32), V((nt, 128, lanes), F32), V((COLS, nt, 8, lanes), F32), V((nt, 128, lanes), F32),
             V((4, nv, lanes), F32), V((4 * nv, nw), F32), V((4 * nv, nw), F32),
-            S(4), S(4, 2), S(4, 2), S(4), S(4), S(4, 5), S(4, 2), S(4, 2, 3), S(4, 2, 2, 2), S(4, 2, 2),
+            S(6), S(4, 2), S(4, 2), S(4), S(4), S(4, 5), S(4, 2), S(4, 2, 3), S(4, 2, 2, 2), S(4, 2, 2),
             S(4), S(4), S(2), S(2), S(2), S(2),
             S(4), S(4), S(4), S(4), S(COLS), S(ROWS, 2), S(4, 2), S(8), S(4, 2, 2), S(COLS), S(ROWS), S(ROWS), S(COLS), S(COLS), S(COLS), S(COLS),
         ]
@@ -537,7 +589,7 @@
         out = pl.pallas_call(
             functools.partial(sweep_kernel, nv),
             out_shape=jax.ShapeDtypeStruct((nw, 4 * nv), F32),
-            in_specs=[vm, vm, vm, hb, hb, hb],
+            in_specs=[vm] + [hb] * 5,
             out_specs=vm,
             scratch_shapes=scratch,
             compiler_params=pltpu.CompilerParams(

time: 124 us -> 120 us (0.968); the launches traced: 124 us -> 118 us
  Pallas kernels: 122 us -> 115 us
    pallas_call x1, Pallas kernels: 122 us -> 115 us  [local(): pl.pallas_call(functools.partial(sweep_kernel, nv), out_shape=jax.ShapeDt...]
where the time goes in v3:
time: 120 us; the launch traced here: 118 us
  Pallas kernels  115 us (96%)
  local copies, waits for them, and re-layouts  2.03 us (2%)
    pallas_call x1, Pallas kernels, local(): pl.pallas_call(functools.partial(sweep_kernel, nv), out_shape=jax.ShapeDt...  115 us

profile of v3, /device:TPU:1, one launch (start us, length us, event | category | flops | bytes accessed | tf_op | source)
XLA Modules:
  0.0 117.5 jit_solution(12512121618307835165)
XLA Ops:
  0.0 115.5 %shard_map.64 = f32[288,576]{1,0:T(8,128)} custom-call(f32[1296,128]{1,0:T(8,128)} %bitcast.9, f32[1296,128]{1,0:T(8,128)} %bitcast.10, bf16[1296,128]{1,0:T(8,128)(2,1)} %bitcast.11, bf16[1296,2592]{1,0:T(8,128)(2,1)} %bitcast.6, bf16[1024,1024]{1,0:T(8,128)(2,1)} %oo_hbm.1, bf16[288,4608]{1,0:T(8,128)(2,1)} %bitcast.8), custom_call_target="tpu_custom_call" | custom-call | tf_op jit(solution)/shard_map/pallas_call | solution.py:589
  115.5 2.0 %copy.8 = f32[576,288]{0,1:T(8,128)} copy(f32[576,288]{0,1:T(8,128)} %bitcast.7) | data formatting | bytes 1327104
